TPU v7x, 32 devices: a whole 2x2x4 slice. The times are simulated.
32 devices in a mesh: depth: 8 (over z, y), lat: 4 (over x, core).
Axes of the slice: x: 2, y: 2, z: 4, core: 2. Of those that a mesh axis runs over, the one named last changes fastest.
Arguments:
- density: bfloat16 [8, 16, 512, 2048], P('depth', None, None, 'lat'), may hold values from 0 to 1
- occupancy: int32 [8, 4, 16], P('depth', None, 'lat'), may hold values from 0 to 1, as said below
- shear_offsets: int32 [8, 16], P('depth'), may hold values from 0 to 127, as said below
- frac_lateral: float32 [8, 16], P('depth'), may hold values from 0.05 to 0.95
- frac_vertical: float32 [8, 16], P('depth'), may hold values from 0.05 to 0.95
- extinction: float32 [8, 16], P('depth'), may hold values from 2 to 32
- slab_gain: float32 [8], P('depth'), may hold values from 0.05 to 1
- view_rank: int32 [8], replicated, may hold values from 0 to 7, as said below
Outputs:
- image_color: float32 [512, 2048], P('depth', 'lat')
- image_alpha: float32 [512, 2048], P('depth', 'lat')
Inputs may be any that keep to these rules, and one draw needn't show every extreme that they name: `occupancy`: A block is 1 if occupied; the share of occupied blocks differs from slab to slab. `shear_offsets`: some slice has the offset 128 - 1. `view_rank`: A permutation of the slabs in which every aligned group of a power of two of slabs holds consecutive ranks.
All inputs are finite; a program needn't handle non-finite values.
Results may differ from a plain program's by a relative error of at most 0.00077.
Values may be sent and summed in bfloat16 or wider, within the bound.
A program may use at most 128 MiB of HBM per device.

v0:
```python
import jax
import jax.numpy as jnp
from jax import lax
from jax.sharding import PartitionSpec as P

SHIFT = 128
BLK = 128


def from_behind(value, axis, steps):
    count = lax.axis_size(axis)
    leading, last = (max(0, -steps), min(count, count - steps))
    return lax.ppermute(value, axis, [(source, source + steps) for source in range(leading, last)])


def partner(value, axis, bit):
    mask = 2**bit
    pairs = [(source, source ^ mask) for source in range(lax.axis_size(axis))]
    return lax.ppermute(value, axis, pairs)


def lateral_weights(offsets, fraction, in_count, out_count):
    source = jnp.arange(in_count, dtype=jnp.int32)[None, :, None]
    target = jnp.arange(out_count, dtype=jnp.int32)[None, None, :]
    shifted = target - offsets[:, None, None]
    first_term = jnp.where(shifted == source, (1.0 - fraction)[:, None, None], 0.0)
    second = jnp.where(shifted - 1 == source, fraction[:, None, None], 0.0)
    return (first_term + second).astype(jnp.bfloat16)


def vertical_weights(fraction, row_count):
    target = jnp.arange(row_count, dtype=jnp.int32)[None, :, None]
    source = jnp.arange(row_count, dtype=jnp.int32)[None, None, :]
    first_term = jnp.where(target == source, (1.0 - fraction)[:, None, None], 0.0)
    second = jnp.where(target - 1 == source, fraction[:, None, None], 0.0)
    return (first_term + second).astype(jnp.bfloat16)


def shade_slices(density_sum, extinction, gain, slice_total):
    row_above = jnp.pad(density_sum, ((0, 0), (1, 0), (0, 0)))[:, :-1, :]
    shading = 0.3 + 0.7 * jax.nn.sigmoid(4.0 * (density_sum - row_above))
    opacity = 1.0 - jnp.exp(-extinction[:, None, None] * density_sum / slice_total)
    emission = opacity * shading * gain
    through = jnp.cumprod(1.0 - opacity, axis=0)
    before = jnp.concatenate([jnp.ones_like(through[:1]), through[:-1]], axis=0)
    return (jnp.sum(emission * before, axis=0), 1.0 - through[-1])


def composite(front_color, front_alpha, back_color, back_alpha):
    return (
        front_color + (1.0 - front_alpha) * back_color,
        front_alpha + (1.0 - front_alpha) * back_alpha,
    )


def shards(
    density, occupancy, shear_offsets, frac_lateral, frac_vertical, extinction, slab_gain, view_rank
):
    slab_voxels = density[0]
    slice_count, row_count, col_count = slab_voxels.shape
    block_rows = row_count // BLK
    block_cols = col_count // BLK
    block_mask = occupancy[0].astype(jnp.bfloat16)
    masked = (
        slab_voxels.reshape(slice_count, block_rows, BLK, block_cols, BLK)
        * block_mask[None, :, None, :, None]
    )
    masked = masked.reshape(slice_count, row_count, col_count)
    lateral_matrix = lateral_weights(
        shear_offsets[0], frac_lateral[0], col_count, col_count + SHIFT
    )
    across = jnp.einsum(
        "srw,swq->srq", masked, lateral_matrix, preferred_element_type=jnp.float32
    ).astype(jnp.bfloat16)
    vertical_matrix = vertical_weights(frac_vertical[0], row_count)
    resampled = jnp.einsum(
        "sij,sjq->siq", vertical_matrix, across, preferred_element_type=jnp.float32
    ).astype(jnp.bfloat16)
    edge_spill = resampled[:, :, col_count:]
    incoming = from_behind(edge_spill, "lat", 1)
    density_sum = resampled[:, :, :col_count].astype(jnp.float32) + jnp.pad(
        incoming.astype(jnp.float32), ((0, 0), (0, 0), (0, col_count - SHIFT))
    )
    slice_total = lax.axis_size("depth") * slice_count
    image_color, image_alpha = shade_slices(density_sum, extinction[0], slab_gain[0], slice_total)
    device_index = lax.axis_index("depth")
    group_size = lax.axis_size("depth")
    piece_rows = row_count // group_size
    my_rank = view_rank[device_index]
    bit_levels = group_size.bit_length() - 1
    held_color = image_color.reshape(group_size, piece_rows, col_count)
    held_alpha = image_alpha.reshape(group_size, piece_rows, col_count)
    for bit_level in range(bit_levels):
        device_bit = device_index >> bit_level & 1
        paired_color = held_color.reshape(held_color.shape[0] // 2, 2, piece_rows, col_count)
        paired_alpha = held_alpha.reshape(held_alpha.shape[0] // 2, 2, piece_rows, col_count)
        keep_color = lax.dynamic_index_in_dim(paired_color, device_bit, 1, keepdims=False)
        keep_alpha = lax.dynamic_index_in_dim(paired_alpha, device_bit, 1, keepdims=False)
        send_color = lax.dynamic_index_in_dim(paired_color, 1 - device_bit, 1, keepdims=False)
        send_alpha = lax.dynamic_index_in_dim(paired_alpha, 1 - device_bit, 1, keepdims=False)
        other_color, other_alpha = partner((send_color, send_alpha), "depth", bit_level)
        in_front = my_rank >> bit_level & 1 == 0
        front_color = jnp.where(in_front, keep_color, other_color)
        front_alpha = jnp.where(in_front, keep_alpha, other_alpha)
        back_color = jnp.where(in_front, other_color, keep_color)
        back_alpha = jnp.where(in_front, other_alpha, keep_alpha)
        held_color, held_alpha = composite(front_color, front_alpha, back_color, back_alpha)
    image_color = held_color.reshape(piece_rows, col_count)
    image_alpha = held_alpha.reshape(piece_rows, col_count)
    return (image_color, image_alpha)


def solution(mesh):
    placed = (
        P("depth", None, None, "lat"),
        P("depth", None, "lat"),
        P("depth", None),
        P("depth", None),
        P("depth", None),
        P("depth", None),
        P("depth"),
        P(),
    )
    return jax.shard_map(
        shards,
        mesh=mesh,
        in_specs=placed,
        out_specs=(P("depth", "lat"), P("depth", "lat")),
        check_vma=False,
    )
```

profile of v0, /device:TPU:2, one launch (start us, length us, event | category | flops | bytes accessed | tf_op | source)
XLA Modules:
  0.0 156.0 jit_solution(875143252288447298)
XLA Ops:
  0.6 0.3 iota_compare_fusion.2
  0.9 0.7 iota_subtract_fusion
  1.7 0.7 convert_bitcast_fusion
  2.4 0.2 mul.66
  2.6 0.1 copy.12
  2.7 0.7 broadcast_subtract_fusion
  3.3 0.0 copy-start.2
  3.3 13.3 %fusion.48 = bf16[16,512,640]{2,1,0:T(8,128)(2,1)} fusion(f32[16]{0:T(128)} %bitcast.97, s32[16,640]{1,0:T(8,128)S(1)} %get-tuple-element.9, f32[16]{0:T(128)S(1)} %get-tuple-element.12, s32[16,640]{1,0:T(8,128)S(1)} %get-tuple-element.8, bf16[1,16,512,512]{3,2,1,0:T(8,128)(2,1)} %param.8, bf16[512,512]{1,0:T(8,128)(2,1)S(1)} %bitcast.95), kind=kOutput, calls=%fused_computation.18.clone.clone.clone.2 | convolution fusion | flops 5409603584 | bytes 19480704 | tf_op jit(solution)/shard_map/srw,swq->srq/dot_general | solution.py:72
  16.6 0.0 copy-done.2
  16.6 0.0 copy-start.3
  16.6 11.1 %fusion.27 = bf16[16,512,640]{2,1,0:T(8,128)(2,1)S(1)} fusion(f32[16]{0:T(128)S(1)} %bitcast.98, f32[16]{0:T(128)S(1)} %get-tuple-element.13, pred[512,512]{1,0:T(8,128)(4,1)S(1)} %get-tuple-element.10, pred[512,512]{1,0:T(8,128)(4,1)S(1)} %get-tuple-element.11, bf16[16,512,640]{2,1,0:T(8,128)(2,1)} %fusion.48), kind=kOutput, calls=%fused_computation.33 | convolution fusion | flops 5390729216 | bytes 21495936 | tf_op jit(solution)/shard_map/sij,sjq->siq/dot_general | solution.py:76
  27.8 0.0 copy-start
  27.8 3.9 %copy-done = bf16[16,512,640]{2,1,0:T(8,128)(2,1)} copy-done((bf16[16,512,640]{2,1,0:T(8,128)(2,1)}, bf16[16,512,640]{2,1,0:T(8,128)(2,1)S(1)}, u32[]{:S(2)}) %copy-start) | copy-done | bytes 10485784
  31.7 1.7 %slice.21 = bf16[16,512,128]{2,1,0:T(8,128)(2,1)} slice(bf16[16,512,640]{2,1,0:T(8,128)(2,1)S(1)} %fusion.27), slice={[0:16], [0:512], [512:640]} | slice | bytes 4194304 | tf_op jit(solution)/shard_map/slice | solution.py:79
  33.4 2.1 %collective-permute-start = (bf16[16,512,128]{2,1,0:T(8,128)(2,1)}, bf16[16,512,128]{2,1,0:T(8,128)(2,1)S(1)}, u32[]{:S(2)}, u32[]{:S(2)}) collective-permute-start(bf16[16,512,128]{2,1,0:T(8,128)(2,1)} %slice.21), channel_id=1, source_target_pairs={{0,1},{1,2},{2,3},{4,5},{5,6},{6,7},{8,9},{9,10},{10,11},{12,13},{... | collective-permute-start | bytes 6291464 | tf_op jit(solution)/shard_map/ppermute | solution.py:13
  36.1 0.0 copy-done.3
  36.2 24.8 %collective-permute-done = bf16[16,512,128]{2,1,0:T(8,128)(2,1)S(1)} collective-permute-done((bf16[16,512,128]{2,1,0:T(8,128)(2,1)}, bf16[16,512,128]{2,1,0:T(8,128)(2,1)S(1)}, u32[]{:S(2)}, u32[]{:S(2)}) %collective-permute-start) | collective-permute-done | bytes 2097184 | tf_op jit(solution)/shard_map/ppermute | solution.py:13
  60.9 10.7 %fusion.6 = f32[16,512,512]{2,1,0:T(8,128)} fusion(f32[16]{0:T(128)S(1)} %negate_bitcast_fusion, bf16[16,512,640]{2,1,0:T(8,128)(2,1)} %copy-done, bf16[16,512,128]{2,1,0:T(8,128)(2,1)S(1)} %collective-permute-done), kind=kOutput, calls=%fused_computation.11 | output fusion | flops 92274688 | bytes 27263040 | tf_op jit(solution)/shard_map/jit(cumprod)/reduce_window | solution.py:44
  71.7 1.3 slice_subtract_fusion
  73.0 13.7 %slice.22 = f32[15,512,512]{2,1,0:T(8,128)} slice(f32[16,512,512]{2,1,0:T(8,128)} %fusion.6), slice={[0:15], [0:512], [0:512]} | slice | bytes 31457280 | tf_op jit(solution)/shard_map/slice | solution.py:45
  86.7 0.9 dynamic-slice_bitcast_fusion
  87.5 1.5 collective-permute-start.2
  89.1 11.6 %convert_add_fusion = f32[16,512,512]{2,1,0:T(8,128)} fusion(bf16[16,512,640]{2,1,0:T(8,128)(2,1)} %copy-done, bf16[16,512,128]{2,1,0:T(8,128)(2,1)S(1)} %collective-permute-done), kind=kLoop, calls=%fused_computation.14 | loop fusion | flops 12582912 | bytes 27262976 | tf_op jit(solution)/shard_map/add | solution.py:81
  100.6 0.0 copy-start.4
  100.6 23.5 %multiply_reduce_fusion = f32[512,512]{1,0:T(8,128)S(1)} fusion(f32[15,512,512]{2,1,0:T(8,128)} %slice.22, f32[16,512,512]{2,1,0:T(8,128)} %convert_add_fusion, f32[]{:T(128)} %bitcast.85, f32[16]{0:T(128)S(1)} %negate_bitcast_fusion), kind=kLoop, calls=%fused_computation.10 | loop fusion | flops 58458112 | bytes 33554500 | tf_op jit(solution)/shard_map/reduce_sum | solution.py:46
  124.2 0.6 collective-permute-start.1
  124.7 0.0 copy-done.4
  124.7 0.6 dynamic_slice.34
  126.0 0.0 collective-permute-done.2
  126.0 7.4 %collective-permute-done.1 = f32[4,64,512]{2,1,0:T(8,128)S(1)} collective-permute-done((f32[4,64,512]{2,1,0:T(8,128)S(1)}, f32[4,64,512]{2,1,0:T(8,128)S(1)}, u32[]{:S(2)}, u32[]{:S(2)}) %collective-permute-start.1) | collective-permute-done | bytes 524320 | tf_op jit(solution)/shard_map/ppermute | solution.py:19
  133.4 0.0 copy-start.1
  133.4 0.8 copy-done.1
  134.2 1.4 fusion.33
  135.7 1.6 %collective-permute-start.4 = (f32[2,64,512]{2,1,0:T(8,128)S(1)}, f32[2,64,512]{2,1,0:T(8,128)S(1)}, u32[]{:S(2)}, u32[]{:S(2)}) collective-permute-start(f32[2,64,512]{2,1,0:T(8,128)S(1)} %dynamic-slice_bitcast_fusion.2), channel_id=1, source_target_pairs={{0,8},{4,12},{8,0},{12,4},{16,24},{20,28},{24,16},{28,20},{1,9},{5... | collective-permute-start | bytes 786440 | tf_op jit(solution)/shard_map/ppermute | solution.py:19
  137.4 0.5 collective-permute-start.3
  138.5 3.6 %collective-permute-done.4 = f32[2,64,512]{2,1,0:T(8,128)S(1)} collective-permute-done((f32[2,64,512]{2,1,0:T(8,128)S(1)}, f32[2,64,512]{2,1,0:T(8,128)S(1)}, u32[]{:S(2)}, u32[]{:S(2)}) %collective-permute-start.4) | collective-permute-done | bytes 262176 | tf_op jit(solution)/shard_map/ppermute | solution.py:19
  142.1 2.8 %collective-permute-done.3 = f32[2,64,512]{2,1,0:T(8,128)S(1)} collective-permute-done((f32[2,64,512]{2,1,0:T(8,128)S(1)}, f32[2,64,512]{2,1,0:T(8,128)S(1)}, u32[]{:S(2)}, u32[]{:S(2)}) %collective-permute-start.3) | collective-permute-done | bytes 262176 | tf_op jit(solution)/shard_map/ppermute | solution.py:19
  145.0 0.1 fusion.37
  145.1 2.6 %collective-permute-start.6 = (f32[1,64,512]{2,1,0:T(8,128)S(1)}, f32[1,64,512]{2,1,0:T(8,128)S(1)}, u32[]{:S(2)}, u32[]{:S(2)}) collective-permute-start(f32[1,64,512]{2,1,0:T(8,128)S(1)} %constant_dynamic-slice_fusion), channel_id=1, source_target_pairs={{0,16},{4,20},{8,24},{12,28},{16,0},{20,4},{24,8},{28,12},{1,17},{... | collective-permute-start | bytes 393224 | tf_op jit(solution)/shard_map/ppermute | solution.py:19
  147.8 0.4 collective-permute-start.5
  148.8 3.6 %collective-permute-done.6 = f32[1,64,512]{2,1,0:T(8,128)S(1)} collective-permute-done((f32[1,64,512]{2,1,0:T(8,128)S(1)}, f32[1,64,512]{2,1,0:T(8,128)S(1)}, u32[]{:S(2)}, u32[]{:S(2)}) %collective-permute-start.6) | collective-permute-done | bytes 131104 | tf_op jit(solution)/shard_map/ppermute | solution.py:19
  152.4 2.8 %collective-permute-done.5 = f32[1,64,512]{2,1,0:T(8,128)S(1)} collective-permute-done((f32[1,64,512]{2,1,0:T(8,128)S(1)}, f32[1,64,512]{2,1,0:T(8,128)S(1)}, u32[]{:S(2)}, u32[]{:S(2)}) %collective-permute-start.5) | collective-permute-done | bytes 131104 | tf_op jit(solution)/shard_map/ppermute | solution.py:19
  155.2 0.7 add_bitcast_fusion
  (7 shorter events, 0.1 us)
Async XLA Ops:
  3.3 13.3 %copy-start.2 = (f32[1,16]{1,0:T(1,128)S(1)}, f32[1,16]{1,0:T(1,128)}, u32[]{:S(2)}) copy-start(f32[1,16]{1,0:T(1,128)} %param.12) | copy-start | bytes 196
  16.6 19.5 %copy-start.3 = (f32[1,16]{1,0:T(1,128)S(1)}, f32[1,16]{1,0:T(1,128)}, u32[]{:S(2)}) copy-start(f32[1,16]{1,0:T(1,128)} %param.13) | copy-start | bytes 196
  27.8 3.9 %copy-start = (bf16[16,512,640]{2,1,0:T(8,128)(2,1)}, bf16[16,512,640]{2,1,0:T(8,128)(2,1)S(1)}, u32[]{:S(2)}) copy-start(bf16[16,512,640]{2,1,0:T(8,128)(2,1)S(1)} %fusion.27) | copy-start | bytes 31457284
  33.4 27.6 %collective-permute-start = (bf16[16,512,128]{2,1,0:T(8,128)(2,1)}, bf16[16,512,128]{2,1,0:T(8,128)(2,1)S(1)}, u32[]{:S(2)}, u32[]{:S(2)}) collective-permute-start(bf16[16,512,128]{2,1,0:T(8,128)(2,1)} %slice.21), channel_id=1, source_target_pairs={{0,1},{1,2},{2,3},{4,5},{5,6},{6,7},{8,9},{9,10},{10,11},{12,13},{... | collective-permute-start | bytes 6291464 | tf_op jit(solution)/shard_map/ppermute | solution.py:13
  87.5 38.4 %collective-permute-start.2 = (f32[4,64,512]{2,1,0:T(8,128)}, f32[4,64,512]{2,1,0:T(8,128)}, u32[]{:S(2)}, u32[]{:S(2)}) collective-permute-start(f32[4,64,512]{2,1,0:T(8,128)} %dynamic-slice_bitcast_fusion), channel_id=1, source_target_pairs={{0,4},{4,0},{8,12},{12,8},{16,20},{20,16},{24,28},{28,24},{1,5},{5... | collective-permute-start | bytes 1572872 | tf_op jit(solution)/shard_map/ppermute | solution.py:19
  100.6 24.1 %copy-start.4 = (s32[8]{0:T(128)S(1)}, s32[8]{0:T(128)}, u32[]{:S(2)}) copy-start(s32[8]{0:T(128)} %param.15) | copy-start | bytes 100
  124.2 9.2 %collective-permute-start.1 = (f32[4,64,512]{2,1,0:T(8,128)S(1)}, f32[4,64,512]{2,1,0:T(8,128)S(1)}, u32[]{:S(2)}, u32[]{:S(2)}) collective-permute-start(f32[4,64,512]{2,1,0:T(8,128)S(1)} %dynamic-slice_bitcast_fusion.1), channel_id=1, source_target_pairs={{0,4},{4,0},{8,12},{12,8},{16,20},{20,16},{24,28},{28,24},{1,5},{5... | collective-permute-start | bytes 1572872 | tf_op jit(solution)/shard_map/ppermute | solution.py:19
  133.4 0.8 copy-start.1
  135.7 6.4 %collective-permute-start.4 = (f32[2,64,512]{2,1,0:T(8,128)S(1)}, f32[2,64,512]{2,1,0:T(8,128)S(1)}, u32[]{:S(2)}, u32[]{:S(2)}) collective-permute-start(f32[2,64,512]{2,1,0:T(8,128)S(1)} %dynamic-slice_bitcast_fusion.2), channel_id=1, source_target_pairs={{0,8},{4,12},{8,0},{12,4},{16,24},{20,28},{24,16},{28,20},{1,9},{5... | collective-permute-start | bytes 786440 | tf_op jit(solution)/shard_map/ppermute | solution.py:19
  137.4 7.6 %collective-permute-start.3 = (f32[2,64,512]{2,1,0:T(8,128)S(1)}, f32[2,64,512]{2,1,0:T(8,128)S(1)}, u32[]{:S(2)}, u32[]{:S(2)}) collective-permute-start(f32[2,64,512]{2,1,0:T(8,128)S(1)} %dynamic-slice_bitcast_fusion.3), channel_id=1, source_target_pairs={{0,8},{4,12},{8,0},{12,4},{16,24},{20,28},{24,16},{28,20},{1,9},{5... | collective-permute-start | bytes 786440 | tf_op jit(solution)/shard_map/ppermute | solution.py:19
  145.1 7.3 %collective-permute-start.6 = (f32[1,64,512]{2,1,0:T(8,128)S(1)}, f32[1,64,512]{2,1,0:T(8,128)S(1)}, u32[]{:S(2)}, u32[]{:S(2)}) collective-permute-start(f32[1,64,512]{2,1,0:T(8,128)S(1)} %constant_dynamic-slice_fusion), channel_id=1, source_target_pairs={{0,16},{4,20},{8,24},{12,28},{16,0},{20,4},{24,8},{28,12},{1,17},{... | collective-permute-start | bytes 393224 | tf_op jit(solution)/shard_map/ppermute | solution.py:19
  147.8 7.5 %collective-permute-start.5 = (f32[1,64,512]{2,1,0:T(8,128)S(1)}, f32[1,64,512]{2,1,0:T(8,128)S(1)}, u32[]{:S(2)}, u32[]{:S(2)}) collective-permute-start(f32[1,64,512]{2,1,0:T(8,128)S(1)} %constant_dynamic-slice_fusion.1), channel_id=1, source_target_pairs={{0,16},{4,20},{8,24},{12,28},{16,0},{20,4},{24,8},{28,12},{1,17},{... | collective-permute-start | bytes 393224 | tf_op jit(solution)/shard_map/ppermute | solution.py:19
where the time goes:
time: 156 us
  other arithmetic  51.8 us (33%)
  waiting for transfers between devices  45 us (29%)
  matrix products  24.4 us (16%)
  local copies, waits for them, and re-layouts  21.9 us (14%)
  starting transfers between devices  9.39 us (6%)
  between operations  3.39 us (2%)
    ppermute x1, waiting for transfers between devices, from_behind(): lax.ppermute(value, axis, [(source, source + steps) for source in range(l...  24.8 us
    reduce_sum x1, other arithmetic, shade_slices(): return (jnp.sum(emission * before, axis=0), 1.0 - through[-1])  23.5 us
    ppermute x6, waiting for transfers between devices, partner(): return lax.ppermute(value, axis, pairs)  20.3 us
    slice x1, local copies, waits for them, and re-layouts, shade_slices(): before = jnp.concatenate([jnp.ones_like(through[:1]), through[:-1]], axis=0)  13.7 us
    dot_general x1, matrix products, shards(): jnp.einsum('srw,swq->srq', masked, lateral_matrix, preferred_element_type...  13.3 us
    add x1, other arithmetic, shards(): resampled[:, :, :col_count].astype(jnp.float32)  11.6 us
    dot_general x1, matrix products, shards(): jnp.einsum('sij,sjq->siq', vertical_matrix, across, preferred_element_typ...  11.1 us
    another operation x1, other arithmetic, shade_slices(): through = jnp.cumprod(1.0 - opacity, axis=0)  10.7 us
  transfers between devices with their start and end apart: 7, of which 6 were waited for; matrix products, arithmetic and copies ran while one was open for 23% of the time, Pallas kernels for 0%

commit v1 on v0

v1 whole, which is shorter than its diff:
```python
import functools
import math

import jax
import jax.numpy as jnp
from jax import lax
from jax.experimental import pallas as pl
from jax.experimental.pallas import tpu as pltpu
from jax.sharding import PartitionSpec as P

SHIFT = 128
BLK = 128
HALO = 16


def rounded(x):
    return x.astype(jnp.bfloat16).astype(jnp.float32)


def build_lateral(lmat, off, prm, slices):
    source = lax.broadcasted_iota(jnp.int32, (2 * SHIFT, SHIFT), 0)
    target = lax.broadcasted_iota(jnp.int32, (2 * SHIFT, SHIFT), 1)
    lag = target + SHIFT - source
    for s in range(slices):
        first = jnp.where(lag == off[0, s], prm[0, s], 0.0)
        second = jnp.where(lag - 1 == off[0, s], prm[1, s], 0.0)
        lmat[s] = (first + second).astype(jnp.bfloat16)


def march(r, left, right, left_occ, left_halo, right_occ, right_halo, lmat, prm, slices):
    row = pl.multiple_of(r * BLK, BLK)
    above = pl.multiple_of(jnp.maximum(r * BLK - HALO, 0), HALO)

    def scaled(ref, s, start, count, by):
        return ref[s, pl.ds(start, count), :] * jnp.full((count, SHIFT), by).astype(jnp.bfloat16)

    through = jnp.ones((BLK, SHIFT), jnp.float32)
    color = jnp.zeros((BLK, SHIFT), jnp.float32)
    for s in range(slices):
        top = jnp.concatenate(
            [scaled(left, s, above, HALO, left_halo), scaled(right, s, above, HALO, right_halo)], 1
        )
        body = jnp.concatenate(
            [scaled(left, s, row, BLK, left_occ), scaled(right, s, row, BLK, right_occ)], 1
        )
        voxels = jnp.concatenate([top, body], 0)
        across = rounded(jnp.dot(voxels, lmat[s], preferred_element_type=jnp.float32))
        field = rounded(prm[2, s] * across + prm[3, s] * pltpu.roll(across, 1, 0))
        slope = (field - pltpu.roll(field, 1, 0))[HALO:]
        after = through * jnp.exp2(prm[4, s] * field[HALO:])
        color = color + (through - after) * jnp.tanh(slope)
        through = after
    return color, through


def finish(color, through, gain):
    alpha = 1.0 - through
    return gain * (0.35 * color + 0.65 * alpha), alpha


def main_kernel(slices, left, right, occ, off, prm, gain, color_out, alpha_out, lmat):
    t, r = pl.program_id(0), pl.program_id(1)

    @pl.when((t == 0) & (r == 0))
    def _():
        build_lateral(lmat, off, prm, slices)

    up = jnp.maximum(r - 1, 0)
    inside = jnp.where(r > 0, 1.0, 0.0)
    color, through = march(
        r, left, right, occ[r, t], occ[up, t] * inside, occ[r, t + 1], occ[up, t + 1] * inside,
        lmat, prm, slices,
    )
    color_out[...], alpha_out[...] = finish(color, through, gain[0])


def edge_kernel(slices, left, right, occ, off, prm, gain, color_out, alpha_out, lmat):
    r = pl.program_id(0)

    @pl.when(r == 0)
    def _():
        build_lateral(lmat, off, prm, slices)

    up = jnp.maximum(r - 1, 0)
    inside = jnp.where(r > 0, 1.0, 0.0)
    color, through = march(
        r, left, right, 1.0, inside, occ[r, 0], occ[up, 0] * inside, lmat, prm, slices
    )
    color_out[...], alpha_out[...] = finish(color, through, gain[0])


def from_behind(value, axis, steps):
    count = lax.axis_size(axis)
    leading, last = (max(0, -steps), min(count, count - steps))
    return lax.ppermute(value, axis, [(source, source + steps) for source in range(leading, last)])


def partner(value, axis, bit):
    mask = 2**bit
    pairs = [(source, source ^ mask) for source in range(lax.axis_size(axis))]
    return lax.ppermute(value, axis, pairs)


def composite(front_color, front_alpha, back_color, back_alpha):
    return (
        front_color + (1.0 - front_alpha) * back_color,
        front_alpha + (1.0 - front_alpha) * back_alpha,
    )


def encode(x):
    return jnp.round(x * 65535.0 - 32768.0).astype(jnp.int16)


def decode(x):
    return (x.astype(jnp.float32) + 32768.0) * (1.0 / 65535.0)


def shards(
    density, occupancy, shear_offsets, frac_lateral, frac_vertical, extinction, slab_gain, view_rank
):
    voxels = density[0]
    slices, rows, cols = voxels.shape
    row_blocks, col_blocks = rows // BLK, cols // SHIFT
    occ = occupancy[0].astype(jnp.float32)
    slice_total = lax.axis_size("depth") * slices
    prm = jnp.stack(
        [
            1.0 - frac_lateral[0],
            frac_lateral[0],
            2.0 * lax.reduce_precision(1.0 - frac_vertical[0], 8, 7),
            2.0 * lax.reduce_precision(frac_vertical[0], 8, 7),
            extinction[0] * (-0.5 * math.log2(math.e) / slice_total),
        ]
    )
    edge_mask = jnp.repeat(occ[:, -1], BLK).astype(jnp.bfloat16)
    edge = from_behind(voxels[:, :, cols - SHIFT :] * edge_mask[None, :, None], "lat", 1)
    smem = pl.BlockSpec(memory_space=pltpu.SMEM)
    tile = (slices, rows, SHIFT)
    scratch = [pltpu.VMEM((slices, 2 * SHIFT, SHIFT), jnp.bfloat16)]
    main_color, main_alpha = pl.pallas_call(
        functools.partial(main_kernel, slices),
        grid=(col_blocks - 1, row_blocks),
        in_specs=[
            pl.BlockSpec(tile, lambda t, r: (0, 0, t)),
            pl.BlockSpec(tile, lambda t, r: (0, 0, t + 1)),
            smem, smem, smem, smem,
        ],
        out_specs=[pl.BlockSpec((BLK, SHIFT), lambda t, r: (r, t))] * 2,
        out_shape=[jax.ShapeDtypeStruct((rows, cols - SHIFT), jnp.float32)] * 2,
        scratch_shapes=scratch,
        cost_estimate=pl.CostEstimate(
            flops=8 * 10**9, bytes_accessed=16 * 2**20, transcendentals=8 * 10**6
        ),
    )(voxels, voxels, occ, shear_offsets, prm, slab_gain)
    edge_color, edge_alpha = pl.pallas_call(
        functools.partial(edge_kernel, slices),
        grid=(row_blocks,),
        in_specs=[
            pl.BlockSpec(tile, lambda r: (0, 0, 0)),
            pl.BlockSpec(tile, lambda r: (0, 0, 0)),
            smem, smem, smem, smem,
        ],
        out_specs=[pl.BlockSpec((BLK, SHIFT), lambda r: (r, 0))] * 2,
        out_shape=[jax.ShapeDtypeStruct((rows, SHIFT), jnp.float32)] * 2,
        scratch_shapes=scratch,
        cost_estimate=pl.CostEstimate(
            flops=3 * 10**9, bytes_accessed=4 * 2**20, transcendentals=2 * 10**6
        ),
    )(edge, voxels, occ, shear_offsets, prm, slab_gain)
    image_color = jnp.concatenate([edge_color, main_color], 1)
    image_alpha = jnp.concatenate([edge_alpha, main_alpha], 1)

    device_index = lax.axis_index("depth")
    group_size = lax.axis_size("depth")
    piece_rows = rows // group_size
    my_rank = view_rank[device_index]
    held = jnp.stack([image_color, image_alpha]).reshape(2, group_size, piece_rows, cols)
    for bit_level in range(group_size.bit_length() - 1):
        device_bit = device_index >> bit_level & 1
        paired = held.reshape(2, held.shape[1] // 2, 2, piece_rows, cols)
        keep = lax.dynamic_index_in_dim(paired, device_bit, 2, keepdims=False)
        send = lax.dynamic_index_in_dim(paired, 1 - device_bit, 2, keepdims=False)
        other = decode(partner(encode(send), "depth", bit_level))
        in_front = my_rank >> bit_level & 1 == 0
        front = jnp.where(in_front, keep, other)
        back = jnp.where(in_front, other, keep)
        held = jnp.stack(composite(front[0], front[1], back[0], back[1]))
    return held[0].reshape(piece_rows, cols), held[1].reshape(piece_rows, cols)


def solution(mesh):
    placed = (
        P("depth", None, None, "lat"),
        P("depth", None, "lat"),
        P("depth", None),
        P("depth", None),
        P("depth", None),
        P("depth", None),
        P("depth"),
        P(),
    )
    return jax.shard_map(
        shards,
        mesh=mesh,
        in_specs=placed,
        out_specs=(P("depth", "lat"), P("depth", "lat")),
        check_vma=False,
    )
```

time: 156 us -> 67.8 us (0.43)
  the two profiles are of different devices: /device:TPU:2 before, /device:TPU:1 now
where the time goes in v1:
time: 67.8 us; the launch traced here: 67.5 us
  Pallas kernels  25.3 us (37%)
  waiting for transfers between devices  20.3 us (30%)
  starting transfers between devices  10.5 us (15%)
  other arithmetic  6.42 us (9%)
  between operations  3.4 us (5%)
  local copies, waits for them, and re-layouts  1.55 us (2%)
    pallas_call x1, Pallas kernels, shards(): pl.pallas_call(functools.partial(main_kernel, slices), grid=(col_blocks -...  18.2 us
    ppermute x3, waiting for transfers between devices, partner(): return lax.ppermute(value, axis, pairs)  16.9 us
    pallas_call x1, Pallas kernels, shards(): pl.pallas_call(functools.partial(edge_kernel, slices), grid=(row_blocks,)...  7.15 us
    ppermute x3, starting transfers between devices, partner(): return lax.ppermute(value, axis, pairs)  5.98 us
    ppermute x1, starting transfers between devices, from_behind(): lax.ppermute(value, axis, [(source, source + steps) for source in range(l...  4.5 us
    ppermute x1, waiting for transfers between devices, from_behind(): lax.ppermute(value, axis, [(source, source + steps) for source in range(l...  3.48 us
    mul x1, other arithmetic, shards(): voxels[:, :, cols - SHIFT:] * edge_mask[None, :, None]  1.85 us
  transfers between devices with their start and end apart: 4, of which 4 were waited for; matrix products, arithmetic and copies ran while one was open for 2% of the time, Pallas kernels for 27%

profile of v1, /device:TPU:1, one launch (start us, length us, event | category | flops | bytes accessed | tf_op | source)
XLA Modules:
  0.0 67.5 jit_solution(13490214550434449174)
XLA Ops:
  0.6 1.3 %fusion.38 = (bf16[4,4]{1,0:T(4,128)(2,1)S(1)}, f32[4,4]{1,0:T(4,128)}) fusion(s32[1,4,4]{2,1,0:T(4,128)} %param.9), kind=kLoop, calls=%fused_computation.73 | loop fusion | flops 32 | bytes 160 | tf_op jit(solution)/shard_map/convert
  1.9 0.2 slice_reduce_fusion
  2.1 0.1 broadcast_bitcast_fusion
  2.2 0.0 copy-start.5
  2.2 0.0 copy-start.3
  2.2 0.0 copy-start.4
  2.2 1.8 %slice_multiply_fusion = bf16[16,512,128]{2,1,0:T(8,128)(2,1)S(1)} fusion(bf16[16,512,512]{2,1,0:T(8,128)(2,1)} %bitcast.78, bf16[512]{0:T(512)(128)(2,1)S(1)} %broadcast_bitcast_fusion), kind=kLoop, calls=%fused_computation.4 | loop fusion | flops 1048576 | bytes 4195328 | tf_op jit(solution)/shard_map/mul | solution.py:137
  4.0 4.5 %collective-permute-start = (bf16[16,512,128]{2,1,0:T(8,128)(2,1)S(1)}, bf16[16,512,128]{2,1,0:T(8,128)(2,1)}, u32[]{:S(2)}, u32[]{:S(2)}) collective-permute-start(bf16[16,512,128]{2,1,0:T(8,128)(2,1)S(1)} %slice_multiply_fusion), channel_id=1, source_target_pairs={{0,1},{1,2},{2,3},{4,5},{5,6},{6,7},{8,9},{9,10},{10,11},{12,13},{... | collective-permute-start | bytes 6291464 | tf_op jit(solution)/shard_map/ppermute | solution.py:95
  9.2 0.0 copy-done.5
  9.2 0.0 copy-done.3
  9.2 0.0 copy-done.4
  9.2 0.6 stack.30.prm
  9.8 18.2 %shard_map.96 = (f32[512,384]{1,0:T(8,128)}, f32[512,384]{1,0:T(8,128)}) custom-call(bf16[16,512,512]{2,1,0:T(8,128)(2,1)} %bitcast.79, bf16[16,512,512]{2,1,0:T(8,128)(2,1)} %bitcast.80, f32[4,4]{1,0:T(4,128)} %get-tuple-element.23.occ, s32[1,16]{1,0:T(1,128)} %off.3, f32[5,16]{1,0:T(8,128)} %stack.30.prm, f32[1]{0:T(128)S(6)} %copy.15.gain), custom_call_target="tpu_custom_call" | custom-call | flops 8000000000 | bytes 16777216 | tf_op jit(solution)/shard_map/pallas_call | solution.py:141
  28.0 0.0 copy-start.1
  28.0 3.5 %collective-permute-done.left = bf16[16,512,128]{2,1,0:T(8,128)(2,1)} collective-permute-done((bf16[16,512,128]{2,1,0:T(8,128)(2,1)S(1)}, bf16[16,512,128]{2,1,0:T(8,128)(2,1)}, u32[]{:S(2)}, u32[]{:S(2)}) %collective-permute-start) | collective-permute-done | bytes 2097184 | tf_op jit(solution)/shard_map/ppermute | solution.py:95
  31.5 7.2 %shard_map.95 = (f32[512,128]{1,0:T(8,128)}, f32[512,128]{1,0:T(8,128)}) custom-call(bf16[16,512,128]{2,1,0:T(8,128)(2,1)} %collective-permute-done.left, bf16[16,512,512]{2,1,0:T(8,128)(2,1)} %bitcast.81, f32[4,4]{1,0:T(4,128)} %get-tuple-element.23.occ, s32[1,16]{1,0:T(1,128)} %off.3, f32[5,16]{1,0:T(8,128)} %stack.30.prm, f32[1]{0:T(128)S(6)} %copy.15.gain), custom_call_target="tpu_custom_call" | custom-call | flops 3000000000 | bytes 4194304 | tf_op jit(solution)/shard_map/pallas_call | solution.py:156
  38.6 0.0 copy-start
  38.6 0.0 copy-start.2
  38.6 0.0 copy-done.1
  38.6 1.2 %pad_maximum_fusion = f32[512,512]{1,0:T(8,128)S(1)} fusion(f32[512,384]{1,0:T(8,128)S(1)} %copy-done.1, f32[512,128]{1,0:T(8,128)} %get-tuple-element.6), kind=kLoop, calls=%fused_computation.17 | loop fusion | flops 262144 | bytes 2097152 | tf_op jit(solution)/shard_map/concatenate | solution.py:171
  39.8 0.0 copy-done
  39.8 0.1 copy-done.2
  39.9 0.0 copy-start.6
  39.9 0.1 pad_maximum_fusion.1
  40.0 0.2 fusion.21
  40.2 1.3 %collective-permute-start.1 = (s16[2,4,64,512]{3,2,1,0:T(8,128)(2,1)S(1)}, s16[2,4,64,512]{3,2,1,0:T(8,128)(2,1)S(1)}, u32[]{:S(2)}, u32[]{:S(2)}) collective-permute-start(s16[2,4,64,512]{3,2,1,0:T(8,128)(2,1)S(1)} %fusion.21), channel_id=1, source_target_pairs={{0,4},{4,0},{8,12},{12,8},{16,20},{20,16},{24,28},{28,24},{1,5},{5... | collective-permute-start | bytes 1572872 | tf_op jit(solution)/shard_map/ppermute | solution.py:101
  41.6 0.0 copy-done.6
  41.6 0.6 dynamic_slice.20
  42.8 7.8 %collective-permute-done.1 = s16[2,4,64,512]{3,2,1,0:T(8,128)(2,1)S(1)} collective-permute-done((s16[2,4,64,512]{3,2,1,0:T(8,128)(2,1)S(1)}, s16[2,4,64,512]{3,2,1,0:T(8,128)(2,1)S(1)}, u32[]{:S(2)}, u32[]{:S(2)}) %collective-permute-start.1) | collective-permute-done | bytes 524320 | tf_op jit(solution)/shard_map/ppermute | solution.py:101
  50.6 0.3 fusion.9
  51.0 0.2 fusion.18
  51.2 0.1 fusion.32
  51.3 1.9 %collective-permute-start.2 = (s16[2,2,64,512]{3,2,1,0:T(8,128)(2,1)S(1)}, s16[2,2,64,512]{3,2,1,0:T(8,128)(2,1)S(1)}, u32[]{:S(2)}, u32[]{:S(2)}) collective-permute-start(s16[2,2,64,512]{3,2,1,0:T(8,128)(2,1)S(1)} %fusion.32), channel_id=1, source_target_pairs={{0,8},{4,12},{8,0},{12,4},{16,24},{20,28},{24,16},{28,20},{1,9},{5... | collective-permute-start | bytes 786440 | tf_op jit(solution)/shard_map/ppermute | solution.py:101
  53.8 3.9 %collective-permute-done.2 = s16[2,2,64,512]{3,2,1,0:T(8,128)(2,1)S(1)} collective-permute-done((s16[2,2,64,512]{3,2,1,0:T(8,128)(2,1)S(1)}, s16[2,2,64,512]{3,2,1,0:T(8,128)(2,1)S(1)}, u32[]{:S(2)}, u32[]{:S(2)}) %collective-permute-start.2) | collective-permute-done | bytes 262176 | tf_op jit(solution)/shard_map/ppermute | solution.py:101
  57.8 0.2 fusion.20
  57.9 0.1 fusion.28
  58.1 0.1 fusion.26
  58.1 2.8 %collective-permute-start.3 = (s16[2,1,64,512]{3,2,1,0:T(8,128)(2,1)S(1)}, s16[2,1,64,512]{3,2,1,0:T(8,128)(2,1)S(1)}, u32[]{:S(2)}, u32[]{:S(2)}) collective-permute-start(s16[2,1,64,512]{3,2,1,0:T(8,128)(2,1)S(1)} %fusion.26), channel_id=1, source_target_pairs={{0,16},{4,20},{8,24},{12,28},{16,0},{20,4},{24,8},{28,12},{1,17},{... | collective-permute-start | bytes 393224 | tf_op jit(solution)/shard_map/ppermute | solution.py:101
  61.6 5.1 %collective-permute-done.3 = s16[2,1,64,512]{3,2,1,0:T(8,128)(2,1)S(1)} collective-permute-done((s16[2,1,64,512]{3,2,1,0:T(8,128)(2,1)S(1)}, s16[2,1,64,512]{3,2,1,0:T(8,128)(2,1)S(1)}, u32[]{:S(2)}, u32[]{:S(2)}) %collective-permute-start.3) | collective-permute-done | bytes 131104 | tf_op jit(solution)/shard_map/ppermute | solution.py:101
  66.7 0.1 fusion.31
  66.8 0.7 %fusion.34 = (f32[64,512]{1,0:T(8,128)}, f32[64,512]{1,0:T(8,128)}) fusion(f32[2,1,64,512]{3,2,1,0:T(8,128)S(1)} %get-tuple-element.19, f32[2,1,64,512]{3,2,1,0:T(8,128)S(1)} %get-tuple-element.18), kind=kLoop, calls=%fused_computation.59 | loop fusion | flops 163840 | bytes 786432 | tf_op jit(solution)/shard_map/add | solution.py:107
  (2 shorter events, 0.0 us)
Async XLA Ops:
  2.2 7.0 %copy-start.5 = (f32[1,16]{1,0:T(1,128)S(1)}, f32[1,16]{1,0:T(1,128)}, u32[]{:S(2)}) copy-start(f32[1,16]{1,0:T(1,128)} %param.12) | copy-start | bytes 196
  2.2 7.0 %copy-start.3 = (f32[1,16]{1,0:T(1,128)S(1)}, f32[1,16]{1,0:T(1,128)}, u32[]{:S(2)}) copy-start(f32[1,16]{1,0:T(1,128)} %param.11) | copy-start | bytes 196
  2.2 7.1 %copy-start.4 = (f32[1,16]{1,0:T(1,128)S(1)}, f32[1,16]{1,0:T(1,128)}, u32[]{:S(2)}) copy-start(f32[1,16]{1,0:T(1,128)} %param.13) | copy-start | bytes 196
  4.0 27.5 %collective-permute-start = (bf16[16,512,128]{2,1,0:T(8,128)(2,1)S(1)}, bf16[16,512,128]{2,1,0:T(8,128)(2,1)}, u32[]{:S(2)}, u32[]{:S(2)}) collective-permute-start(bf16[16,512,128]{2,1,0:T(8,128)(2,1)S(1)} %slice_multiply_fusion), channel_id=1, source_target_pairs={{0,1},{1,2},{2,3},{4,5},{5,6},{6,7},{8,9},{9,10},{10,11},{12,13},{... | collective-permute-start | bytes 6291464 | tf_op jit(solution)/shard_map/ppermute | solution.py:95
  28.0 10.6 %copy-start.1 = (f32[512,384]{1,0:T(8,128)S(1)}, f32[512,384]{1,0:T(8,128)}, u32[]{:S(2)}) copy-start(f32[512,384]{1,0:T(8,128)} %get-tuple-element.7) | copy-start | bytes 2359300
  38.6 1.2 %copy-start = (f32[512,384]{1,0:T(8,128)S(1)}, f32[512,384]{1,0:T(8,128)}, u32[]{:S(2)}) copy-start(f32[512,384]{1,0:T(8,128)} %get-tuple-element.9) | copy-start | bytes 2359300
  38.6 1.3 %copy-start.2 = (f32[512,128]{1,0:T(8,128)S(1)}, f32[512,128]{1,0:T(8,128)}, u32[]{:S(2)}) copy-start(f32[512,128]{1,0:T(8,128)} %get-tuple-element.8) | copy-start | bytes 786436
  39.9 1.7 %copy-start.6 = (s32[8]{0:T(128)S(1)}, s32[8]{0:T(128)}, u32[]{:S(2)}) copy-start(s32[8]{0:T(128)} %param.15) | copy-start | bytes 100
  40.2 10.4 %collective-permute-start.1 = (s16[2,4,64,512]{3,2,1,0:T(8,128)(2,1)S(1)}, s16[2,4,64,512]{3,2,1,0:T(8,128)(2,1)S(1)}, u32[]{:S(2)}, u32[]{:S(2)}) collective-permute-start(s16[2,4,64,512]{3,2,1,0:T(8,128)(2,1)S(1)} %fusion.21), channel_id=1, source_target_pairs={{0,4},{4,0},{8,12},{12,8},{16,20},{20,16},{24,28},{28,24},{1,5},{5... | collective-permute-start | bytes 1572872 | tf_op jit(solution)/shard_map/ppermute | solution.py:101
  51.3 6.5 %collective-permute-start.2 = (s16[2,2,64,512]{3,2,1,0:T(8,128)(2,1)S(1)}, s16[2,2,64,512]{3,2,1,0:T(8,128)(2,1)S(1)}, u32[]{:S(2)}, u32[]{:S(2)}) collective-permute-start(s16[2,2,64,512]{3,2,1,0:T(8,128)(2,1)S(1)} %fusion.32), channel_id=1, source_target_pairs={{0,8},{4,12},{8,0},{12,4},{16,24},{20,28},{24,16},{28,20},{1,9},{5... | collective-permute-start | bytes 786440 | tf_op jit(solution)/shard_map/ppermute | solution.py:101
  58.1 8.6 %collective-permute-start.3 = (s16[2,1,64,512]{3,2,1,0:T(8,128)(2,1)S(1)}, s16[2,1,64,512]{3,2,1,0:T(8,128)(2,1)S(1)}, u32[]{:S(2)}, u32[]{:S(2)}) collective-permute-start(s16[2,1,64,512]{3,2,1,0:T(8,128)(2,1)S(1)} %fusion.26), channel_id=1, source_target_pairs={{0,16},{4,20},{8,24},{12,28},{16,0},{20,4},{24,8},{28,12},{1,17},{... | collective-permute-start | bytes 393224 | tf_op jit(solution)/shard_map/ppermute | solution.py:101

commit v2 on v1

v2 whole, which is shorter than its diff:
```python
import functools
import math

import jax
import jax.numpy as jnp
from jax import lax
from jax.experimental import pallas as pl
from jax.experimental.pallas import tpu as pltpu
from jax.sharding import PartitionSpec as P

SHIFT = 128
BLK = 128
HALO = 16


def rounded(x):
    return x.astype(jnp.bfloat16).astype(jnp.float32)


def build_lateral(lmat, off, prm, slices):
    source = lax.broadcasted_iota(jnp.int32, (2 * SHIFT, SHIFT), 0)
    target = lax.broadcasted_iota(jnp.int32, (2 * SHIFT, SHIFT), 1)
    lag = target + SHIFT - source
    for s in range(slices):
        first = jnp.where(lag == off[0, s], prm[0, s], 0.0)
        second = jnp.where(lag - 1 == off[0, s], prm[1, s], 0.0)
        lmat[s] = (first + second).astype(jnp.bfloat16)


def march(r, left, right, masks, lmat, prm, slices):
    row = pl.multiple_of(r * BLK, BLK)
    above = pl.multiple_of(jnp.maximum(r * BLK - HALO, 0), HALO)
    left_occ, left_halo, right_occ, right_halo = [
        jnp.broadcast_to(mask, (HALO, SHIFT)).astype(jnp.bfloat16) for mask in masks
    ]

    def scaled(read, s, start, count, by):
        return read(s, start, count) * jnp.concatenate([by] * (count // HALO), 0)

    through = jnp.ones((BLK, SHIFT), jnp.float32)
    color = jnp.zeros((BLK, SHIFT), jnp.float32)
    for s in range(slices):
        top = jnp.concatenate(
            [scaled(left, s, above, HALO, left_halo), scaled(right, s, above, HALO, right_halo)], 1
        )
        body = jnp.concatenate(
            [scaled(left, s, row, BLK, left_occ), scaled(right, s, row, BLK, right_occ)], 1
        )
        voxels = jnp.concatenate([top, body], 0)
        across = rounded(jnp.dot(voxels, lmat[s], preferred_element_type=jnp.float32))
        field = rounded(prm[2, s] * across + prm[3, s] * pltpu.roll(across, 1, 0))
        slope = (field - pltpu.roll(field, 1, 0))[HALO:]
        after = through * jnp.exp2(prm[4, s] * field[HALO:])
        color = color + (through - after) * jnp.tanh(slope)
        through = after
    return color, through


def finish(color, through, gain):
    alpha = 1.0 - through
    return gain * (0.35 * color + 0.65 * alpha), alpha


def encode(x):
    return jnp.floor(x * 65535.0 - 32767.5).astype(jnp.int32).astype(jnp.int16)


def decode(x):
    return (x.astype(jnp.int32).astype(jnp.float32) + 32768.0) * (1.0 / 65535.0)


def over(in_front, keep, other):
    keep_color, keep_alpha = keep
    other_color, other_alpha = other
    front_color = jnp.where(in_front, keep_color, other_color)
    front_alpha = jnp.where(in_front, keep_alpha, other_alpha)
    back_color = jnp.where(in_front, other_color, keep_color)
    back_alpha = jnp.where(in_front, other_alpha, keep_alpha)
    return (
        front_color + (1.0 - front_alpha) * back_color,
        front_alpha + (1.0 - front_alpha) * back_alpha,
    )


def render_kernel(
    dims,
    density, occ_edge, occ, off, prm, gain, view_rank,
    color_out, alpha_out,
    voxels, edge, occ_left, lmat, held, first_out, first_in, later_out, later_in,
    load_sem, edge_send, edge_recv, occ_send, occ_recv, first_send, first_recv,
    later_send, later_recv,
):
    slices, rows, cols, group, lanes = dims
    row_blocks, col_blocks = rows // BLK, cols // SHIFT
    piece = rows // group
    pairs = BLK // (2 * piece)
    levels = group.bit_length() - 1
    me, lat = lax.axis_index("depth"), lax.axis_index("lat")
    has_left, has_right = lat > 0, lat < lanes - 1
    my_rank = view_rank[me]

    def depth_id(level):
        return {"depth": me ^ (1 << level), "lat": lat}

    def bit(level):
        return (me >> level) & 1

    def in_front(level):
        return ((my_rank >> level) & 1) == 0

    barrier = pltpu.get_barrier_semaphore()
    for level in range(levels):
        pl.semaphore_signal(
            barrier, inc=1, device_id=depth_id(level), device_id_type=pl.DeviceIdType.MESH
        )

    right_id = {"depth": me, "lat": jnp.minimum(lat + 1, lanes - 1)}
    left_id = {"depth": me, "lat": jnp.maximum(lat - 1, 0)}

    @pl.when(has_left)
    def _():
        pl.semaphore_signal(barrier, inc=1, device_id=left_id, device_id_type=pl.DeviceIdType.MESH)

    @pl.when(has_right)
    def _():
        pl.semaphore_signal(barrier, inc=1, device_id=right_id, device_id_type=pl.DeviceIdType.MESH)

    def load(r):
        span = pl.ds(pl.multiple_of(r * BLK, BLK), BLK)
        return pltpu.make_async_copy(
            density.at[:, span, :], voxels.at[:, span, :], load_sem.at[r]
        )

    def edge_copy(r):
        span = pl.ds(pl.multiple_of(r * BLK, BLK), BLK)
        return pltpu.make_async_remote_copy(
            src_ref=density.at[:, span, pl.ds(cols - SHIFT, SHIFT)],
            dst_ref=edge.at[:, span, :],
            send_sem=edge_send.at[r],
            recv_sem=edge_recv.at[r],
            device_id=right_id,
            device_id_type=pl.DeviceIdType.MESH,
        )

    occ_copy = pltpu.make_async_remote_copy(
        src_ref=occ_edge,
        dst_ref=occ_left,
        send_sem=occ_send,
        recv_sem=occ_recv,
        device_id=right_id,
        device_id_type=pl.DeviceIdType.MESH,
    )

    def first_copy(r):
        return pltpu.make_async_remote_copy(
            src_ref=first_out.at[r],
            dst_ref=first_in.at[r],
            send_sem=first_send.at[r],
            recv_sem=first_recv.at[r],
            device_id=depth_id(0),
            device_id_type=pl.DeviceIdType.MESH,
        )

    for r in range(row_blocks):
        load(r).start()

    @pl.when(jnp.logical_not(has_left))
    def _():
        edge[...] = jnp.zeros_like(edge)
        occ_left[...] = jnp.zeros_like(occ_left)

    build_lateral(lmat, off, prm, slices)

    wanted = levels + has_left.astype(jnp.int32) + has_right.astype(jnp.int32)
    pl.semaphore_wait(barrier, wanted)

    @pl.when(has_right)
    def _():
        occ_copy.start()
        for r in range(row_blocks):
            edge_copy(r).start()

    odd = bit(0) == 1
    zero = jnp.zeros((1, SHIFT), jnp.float32)

    def read_voxels(t):
        def read(s, start, count):
            return voxels[s, pl.ds(start, count), pl.ds(pl.multiple_of(t * SHIFT, SHIFT), SHIFT)]
        return read

    def read_edge(s, start, count):
        return edge[s, pl.ds(start, count), :]

    def tile(r, t, left, left_mask, left_halo):
        up = jnp.maximum(r - 1, 0)
        inside = jnp.where(r > 0, 1.0, 0.0)
        masks = (left_mask, left_halo * inside, zero + occ[r, t], zero + occ[up, t] * inside)
        result = finish(*march(r, left, read_voxels(t), masks, lmat, prm, slices), gain[0])
        lane = pl.ds(pl.multiple_of(t * SHIFT, SHIFT), SHIFT)
        for channel in range(2):
            for k in range(pairs):
                low = result[channel][2 * k * piece : (2 * k + 1) * piece]
                high = result[channel][(2 * k + 1) * piece : (2 * k + 2) * piece]
                held[channel, r * pairs + k, :, lane] = jnp.where(odd, high, low)
                first_out[r, channel, k, :, lane] = encode(jnp.where(odd, low, high))

    def first_merge(r):
        first_copy(r).wait()
        for k in range(pairs):
            keep = held[0, r * pairs + k], held[1, r * pairs + k]
            other = decode(first_in[r, 0, k]), decode(first_in[r, 1, k])
            held[0, r * pairs + k], held[1, r * pairs + k] = over(in_front(0), keep, other)

    def row_step(r, carry):
        load(r).wait()

        def col_step(t, inner):
            up = jnp.maximum(r - 1, 0)
            tile(r, t, read_voxels(t - 1), zero + occ[r, t - 1], zero + occ[up, t - 1])
            return inner

        lax.fori_loop(1, col_blocks, col_step, 0)

        @pl.when(has_left & (r == 0))
        def _():
            occ_copy.wait_recv()

        @pl.when(has_left)
        def _():
            edge_copy(r).wait_recv()

        up = jnp.maximum(r - 1, 0)
        tile(r, 0, read_edge, occ_left[pl.ds(r, 1), :], occ_left[pl.ds(up, 1), :])
        first_copy(r).start()

        @pl.when(r > 0)
        def _():
            first_merge(r - 1)

        return carry

    lax.fori_loop(0, row_blocks, row_step, 0)

    @pl.when(has_right)
    def _():
        occ_copy.wait_send()
        for r in range(row_blocks):
            edge_copy(r).wait_send()

    first_merge(row_blocks - 1)

    slot = 0
    for level in range(1, levels):
        count = group >> (level + 1)

        def later_copy(i):
            return pltpu.make_async_remote_copy(
                src_ref=later_out.at[slot + i],
                dst_ref=later_in.at[slot + i],
                send_sem=later_send.at[slot + i],
                recv_sem=later_recv.at[slot + i],
                device_id=depth_id(level),
                device_id_type=pl.DeviceIdType.MESH,
            )

        for i in range(count):
            away = 2 * i + 1 - bit(level)
            for channel in range(2):
                later_out[slot + i, channel] = encode(held[channel, away])
            later_copy(i).start()
        for i in range(count):
            stay = 2 * i + bit(level)
            later_copy(i).wait()
            keep = held[0, stay], held[1, stay]
            other = decode(later_in[slot + i, 0]), decode(later_in[slot + i, 1])
            held[0, i], held[1, i] = over(in_front(level), keep, other)
        slot += count

    color_out[...] = held[0, 0]
    alpha_out[...] = held[1, 0]


def shards(
    density, occupancy, shear_offsets, frac_lateral, frac_vertical, extinction, slab_gain, view_rank
):
    voxels = density[0]
    slices, rows, cols = voxels.shape
    row_blocks = rows // BLK
    group, lanes = lax.axis_size("depth"), lax.axis_size("lat")
    piece = rows // group
    pairs = BLK // (2 * piece)
    occ = occupancy[0].astype(jnp.float32)
    slice_total = group * slices
    prm = jnp.stack(
        [
            1.0 - frac_lateral[0],
            frac_lateral[0],
            2.0 * lax.reduce_precision(1.0 - frac_vertical[0], 8, 7),
            2.0 * lax.reduce_precision(frac_vertical[0], 8, 7),
            extinction[0] * (-0.5 * math.log2(math.e) / slice_total),
        ]
    )
    pad_rows = -row_blocks % 8
    occ_edge = jnp.broadcast_to(jnp.pad(occ[:, -1:], ((0, pad_rows), (0, 0))), (row_blocks + pad_rows, SHIFT))
    smem = pl.BlockSpec(memory_space=pltpu.SMEM)
    vmem = pl.BlockSpec(memory_space=pltpu.VMEM)
    later = group // 2 - 1
    dma = pltpu.SemaphoreType.DMA
    return pl.pallas_call(
        functools.partial(render_kernel, (slices, rows, cols, group, lanes)),
        in_specs=[pl.BlockSpec(memory_space=pl.ANY), vmem, smem, smem, smem, smem, smem],
        out_specs=[vmem, vmem],
        out_shape=[jax.ShapeDtypeStruct((piece, cols), jnp.float32)] * 2,
        scratch_shapes=[
            pltpu.VMEM((slices, rows, cols), jnp.bfloat16),
            pltpu.VMEM((slices, rows, SHIFT), jnp.bfloat16),
            pltpu.VMEM((row_blocks + pad_rows, SHIFT), jnp.float32),
            pltpu.VMEM((slices, 2 * SHIFT, SHIFT), jnp.bfloat16),
            pltpu.VMEM((2, group // 2, piece, cols), jnp.float32),
            pltpu.VMEM((row_blocks, 2, pairs, piece, cols), jnp.int16),
            pltpu.VMEM((row_blocks, 2, pairs, piece, cols), jnp.int16),
            pltpu.VMEM((later, 2, piece, cols), jnp.int16),
            pltpu.VMEM((later, 2, piece, cols), jnp.int16),
            dma((row_blocks,)),
            dma((row_blocks,)),
            dma((row_blocks,)),
            dma,
            dma,
            dma((row_blocks,)),
            dma((row_blocks,)),
            dma((later,)),
            dma((later,)),
        ],
        compiler_params=pltpu.CompilerParams(
            collective_id=0, has_side_effects=True, vmem_limit_bytes=48 * 2**20
        ),
    )(voxels, occ_edge, occ, shear_offsets, prm, slab_gain, view_rank)


def solution(mesh):
    placed = (
        P("depth", None, None, "lat"),
        P("depth", None, "lat"),
        P("depth", None),
        P("depth", None),
        P("depth", None),
        P("depth", None),
        P("depth"),
        P(),
    )
    return jax.shard_map(
        shards,
        mesh=mesh,
        in_specs=placed,
        out_specs=(P("depth", "lat"), P("depth", "lat")),
        check_vma=False,
    )
```

time: 67.8 us -> 52.3 us (0.77)
  the two profiles are of different devices: /device:TPU:1 before, /device:TPU:2 now
where the time goes in v2:
time: 52.3 us; the launch traced here: 52.1 us
  Pallas kernels  45.2 us (86%)
  local copies, waits for them, and re-layouts  3.56 us (7%)
  other arithmetic  2.02 us (4%)
  between operations  1.29 us (2%)
    pallas_call x1, Pallas kernels, shards(): pl.pallas_call(functools.partial(render_kernel, (slices, rows, cols, grou...  45.2 us
    unnamed x6, local copies, waits for them, and re-layouts  2.62 us

profile of v2, /device:TPU:2, one launch (start us, length us, event | category | flops | bytes accessed | tf_op | source)
XLA Modules:
  0.0 52.1 jit_solution(17570213127030846041)
XLA Ops:
  1.3 0.7 %broadcast_subtract_fusion = f32[1,16]{1,0:T(1,128)S(1)} fusion(f32[1,16]{1,0:T(1,128)} %param.11), kind=kLoop, calls=%fused_computation.5 | loop fusion | flops 16 | bytes 128 | tf_op jit(solution)/shard_map/sub | solution.py:296
  1.9 0.7 %reduce-precision_multiply_fusion = (f32[1,16]{1,0:T(1,128)S(1)}, f32[1,16]{1,0:T(1,128)S(1)}, f32[1,16]{1,0:T(1,128)S(1)}) fusion(f32[1,16]{1,0:T(1,128)} %param.12, f32[1,16]{1,0:T(1,128)} %param.13), kind=kLoop, calls=%fused_computation.2 | loop fusion | flops 96 | bytes 320 | tf_op jit(solution)/shard_map/mul | solution.py:299
  2.6 0.7 %convert_bitcast_fusion.occ = f32[4,4]{1,0:T(4,128)S(1)} fusion(s32[1,4,4]{2,1,0:T(4,128)} %param.9), kind=kLoop, calls=%fused_computation.1 | loop fusion | flops 16 | bytes 128 | tf_op jit(solution)/shard_map/convert_element_type | solution.py:292
  3.3 0.1 slice.3
  3.4 0.1 pad_reduce_fusion
  3.5 0.7 %stack.2.prm = f32[5,16]{1,0:T(8,128)S(1)} concatenate(f32[1,16]{1,0:T(1,128)S(1)} %broadcast_subtract_fusion, f32[1,16]{1,0:T(1,128)} %param.11, f32[1,16]{1,0:T(1,128)S(1)} %get-tuple-element.3, f32[1,16]{1,0:T(1,128)S(1)} %get-tuple-element.2, f32[1,16]{1,0:T(1,128)S(1)} %get-tuple-element.4), dimensions={0} | concatenate | bytes 640 | tf_op jit(solution)/shard_map/stack | solution.py:294
  4.2 0.1 broadcast_in_dim.8.occ_edge
  4.2 0.0 copy-start
  4.2 0.7 %copy-done = s32[1,16]{1,0:T(1,128)S(1)} copy-done((s32[1,16]{1,0:T(1,128)S(1)}, s32[1,16]{1,0:T(1,128)}, u32[]{:S(2)}) %copy-start) | copy-done | bytes 88
  4.9 0.0 copy-start.1
  4.9 0.7 %copy-done.1 = s32[8]{0:T(128)S(1)} copy-done((s32[8]{0:T(128)S(1)}, s32[8]{0:T(128)}, u32[]{:S(2)}) %copy-start.1) | copy-done | bytes 56
  5.5 45.2 %shard_map.95 = (f32[64,512]{1,0:T(8,128)S(1)}, f32[64,512]{1,0:T(8,128)S(1)}) custom-call(bf16[16,512,512]{2,1,0:T(8,128)(2,1)} %bitcast.3, f32[8,128]{1,0:T(8,128)S(1)} %broadcast_in_dim.8.occ_edge, f32[4,4]{1,0:T(4,128)S(1)} %convert_bitcast_fusion.occ, s32[1,16]{1,0:T(1,128)S(1)} %copy-done, f32[5,16]{1,0:T(8,128)S(1)} %stack.2.prm, f32[1]{0:T(128)S(6)} %copy.12.gain, ...), custom_call_target="tpu_custom_call" | custom-call | tf_op jit(solution)/shard_map/pallas_call | solution.py:309
  50.8 0.7 %copy.13 = f32[64,512]{1,0:T(8,128)} copy(f32[64,512]{1,0:T(8,128)S(1)} %get-tuple-element.7) | data formatting | bytes 262144
  51.4 0.7 %copy.14 = f32[64,512]{1,0:T(8,128)} copy(f32[64,512]{1,0:T(8,128)S(1)} %get-tuple-element.8) | data formatting | bytes 262144
Async XLA Ops:
  4.2 0.7 %copy-start = (s32[1,16]{1,0:T(1,128)S(1)}, s32[1,16]{1,0:T(1,128)}, u32[]{:S(2)}) copy-start(s32[1,16]{1,0:T(1,128)} %off.1) | copy-start | bytes 196
  4.9 0.7 %copy-start.1 = (s32[8]{0:T(128)S(1)}, s32[8]{0:T(128)}, u32[]{:S(2)}) copy-start(s32[8]{0:T(128)} %view_rank.1) | copy-start | bytes 100

commit v3 on v2

--- a/solution.py
+++ b/solution.py
@@ -17,17 +17,21 @@
     return x.astype(jnp.bfloat16).astype(jnp.float32)
 
 
-def build_lateral(lmat, off, prm, slices):
+def build_weights(lmat, vertical, off, frac_lateral, frac_vertical, slices):
     source = lax.broadcasted_iota(jnp.int32, (2 * SHIFT, SHIFT), 0)
     target = lax.broadcasted_iota(jnp.int32, (2 * SHIFT, SHIFT), 1)
     lag = target + SHIFT - source
     for s in range(slices):
-        first = jnp.where(lag == off[0, s], prm[0, s], 0.0)
-        second = jnp.where(lag - 1 == off[0, s], prm[1, s], 0.0)
+        part = frac_lateral[0, s]
+        first = jnp.where(lag == off[0, s], 1.0 - part, 0.0)
+        second = jnp.where(lag - 1 == off[0, s], part, 0.0)
         lmat[s] = (first + second).astype(jnp.bfloat16)
-
-
-def march(r, left, right, masks, lmat, prm, slices):
+        down = frac_vertical[0, s]
+        vertical[0, s] = 2.0 * rounded(jnp.full((HALO, SHIFT), 1.0 - down))
+        vertical[1, s] = 2.0 * rounded(jnp.full((HALO, SHIFT), down))
+
+
+def march(r, left, right, masks, lmat, vertical, extinction, scale, slices):
     row = pl.multiple_of(r * BLK, BLK)
     above = pl.multiple_of(jnp.maximum(r * BLK - HALO, 0), HALO)
     left_occ, left_halo, right_occ, right_halo = [
@@ -48,9 +52,11 @@
         )
         voxels = jnp.concatenate([top, body], 0)
         across = rounded(jnp.dot(voxels, lmat[s], preferred_element_type=jnp.float32))
-        field = rounded(prm[2, s] * across + prm[3, s] * pltpu.roll(across, 1, 0))
+        stay = jnp.concatenate([vertical[0, s]] * (BLK // HALO + 1), 0)
+        fall = jnp.concatenate([vertical[1, s]] * (BLK // HALO + 1), 0)
+        field = rounded(stay * across + fall * pltpu.roll(across, 1, 0))
         slope = (field - pltpu.roll(field, 1, 0))[HALO:]
-        after = through * jnp.exp2(prm[4, s] * field[HALO:])
+        after = through * jnp.exp2((extinction[0, s] * scale) * field[HALO:])
         color = color + (through - after) * jnp.tanh(slope)
         through = after
     return color, through
@@ -84,20 +90,22 @@
 
 def render_kernel(
     dims,
-    density, occ_edge, occ, off, prm, gain, view_rank,
+    density, occupancy_in, off_in, frac_lateral_in, frac_vertical_in, extinction_in, rank_in, gain,
     color_out, alpha_out,
-    voxels, edge, occ_left, lmat, held, first_out, first_in, later_out, later_in,
+    occupancy, off, frac_lateral, frac_vertical, extinction, view_rank,
+    voxels, edge, occ_edge, occ_left, lmat, vertical, held, first_out, first_in, later_out, later_in,
     load_sem, edge_send, edge_recv, occ_send, occ_recv, first_send, first_recv,
-    later_send, later_recv,
+    later_send, later_recv, small_sem,
 ):
     slices, rows, cols, group, lanes = dims
     row_blocks, col_blocks = rows // BLK, cols // SHIFT
     piece = rows // group
     pairs = BLK // (2 * piece)
     levels = group.bit_length() - 1
+    early = pairs == 1 and levels > 1
+    scale = -0.5 * math.log2(math.e) / (group * slices)
     me, lat = lax.axis_index("depth"), lax.axis_index("lat")
     has_left, has_right = lat > 0, lat < lanes - 1
-    my_rank = view_rank[me]
 
     def depth_id(level):
         return {"depth": me ^ (1 << level), "lat": lat}
@@ -106,7 +114,23 @@
         return (me >> level) & 1
 
     def in_front(level):
-        return ((my_rank >> level) & 1) == 0
+        return ((view_rank[me] >> level) & 1) == 0
+
+    small = [
+        pltpu.make_async_copy(source, target, small_sem.at[k])
+        for k, (source, target) in enumerate(
+            [
+                (occupancy_in, occupancy),
+                (off_in, off),
+                (frac_lateral_in, frac_lateral),
+                (frac_vertical_in, frac_vertical),
+                (extinction_in, extinction),
+                (rank_in, view_rank),
+            ]
+        )
+    ]
+    for copy in small:
+        copy.start()
 
     barrier = pltpu.get_barrier_semaphore()
     for level in range(levels):
@@ -161,15 +185,25 @@
             device_id_type=pl.DeviceIdType.MESH,
         )
 
+    def occ(r, t):
+        return occupancy[0, r, t].astype(jnp.float32)
+
     for r in range(row_blocks):
         load(r).start()
 
+    for copy in small:
+        copy.wait()
+
+    occ_edge[...] = jnp.zeros_like(occ_edge)
+    for r in range(row_blocks):
+        occ_edge[pl.ds(r, 1), :] = jnp.full((1, SHIFT), occ(r, col_blocks - 1))
+
     @pl.when(jnp.logical_not(has_left))
     def _():
         edge[...] = jnp.zeros_like(edge)
         occ_left[...] = jnp.zeros_like(occ_left)
 
-    build_lateral(lmat, off, prm, slices)
+    build_weights(lmat, vertical, off, frac_lateral, frac_vertical, slices)
 
     wanted = levels + has_left.astype(jnp.int32) + has_right.astype(jnp.int32)
     pl.semaphore_wait(barrier, wanted)
@@ -194,8 +228,8 @@
     def tile(r, t, left, left_mask, left_halo):
         up = jnp.maximum(r - 1, 0)
         inside = jnp.where(r > 0, 1.0, 0.0)
-        masks = (left_mask, left_halo * inside, zero + occ[r, t], zero + occ[up, t] * inside)
-        result = finish(*march(r, left, read_voxels(t), masks, lmat, prm, slices), gain[0])
+        masks = (left_mask, left_halo * inside, zero + occ(r, t), zero + occ(up, t) * inside)
+        result = finish(*march(r, left, read_voxels(t), masks, lmat, vertical, extinction, scale, slices), gain[0])
         lane = pl.ds(pl.multiple_of(t * SHIFT, SHIFT), SHIFT)
         for channel in range(2):
             for k in range(pairs):
@@ -211,12 +245,28 @@
             other = decode(first_in[r, 0, k]), decode(first_in[r, 1, k])
             held[0, r * pairs + k], held[1, r * pairs + k] = over(in_front(0), keep, other)
 
+    def later_copy(level, slot):
+        return pltpu.make_async_remote_copy(
+            src_ref=later_out.at[slot],
+            dst_ref=later_in.at[slot],
+            send_sem=later_send.at[slot],
+            recv_sem=later_recv.at[slot],
+            device_id=depth_id(level),
+            device_id_type=pl.DeviceIdType.MESH,
+        )
+
+    def later_start(level, slot, i):
+        away = 2 * i + 1 - bit(level)
+        for channel in range(2):
+            later_out[slot, channel] = encode(held[channel, away])
+        later_copy(level, slot).start()
+
     def row_step(r, carry):
         load(r).wait()
 
         def col_step(t, inner):
             up = jnp.maximum(r - 1, 0)
-            tile(r, t, read_voxels(t - 1), zero + occ[r, t - 1], zero + occ[up, t - 1])
+            tile(r, t, read_voxels(t - 1), zero + occ(r, t - 1), zero + occ(up, t - 1))
             return inner
 
         lax.fori_loop(1, col_blocks, col_step, 0)
@@ -237,6 +287,12 @@
         def _():
             first_merge(r - 1)
 
+        if early:
+
+            @pl.when((r > 0) & (r % 2 == 0))
+            def _():
+                later_start(1, r // 2 - 1, r // 2 - 1)
+
         return carry
 
     lax.fori_loop(0, row_blocks, row_step, 0)
@@ -252,25 +308,12 @@
     slot = 0
     for level in range(1, levels):
         count = group >> (level + 1)
-
-        def later_copy(i):
-            return pltpu.make_async_remote_copy(
-                src_ref=later_out.at[slot + i],
-                dst_ref=later_in.at[slot + i],
-                send_sem=later_send.at[slot + i],
-                recv_sem=later_recv.at[slot + i],
-                device_id=depth_id(level),
-                device_id_type=pl.DeviceIdType.MESH,
-            )
-
         for i in range(count):
-            away = 2 * i + 1 - bit(level)
-            for channel in range(2):
-                later_out[slot + i, channel] = encode(held[channel, away])
-            later_copy(i).start()
+            if not (early and level == 1 and i < count - 1):
+                later_start(level, slot + i, i)
         for i in range(count):
             stay = 2 * i + bit(level)
-            later_copy(i).wait()
+            later_copy(level, slot + i).wait()
             keep = held[0, stay], held[1, stay]
             other = decode(later_in[slot + i, 0]), decode(later_in[slot + i, 1])
             held[0, i], held[1, i] = over(in_front(level), keep, other)
@@ -289,33 +332,27 @@
     group, lanes = lax.axis_size("depth"), lax.axis_size("lat")
     piece = rows // group
     pairs = BLK // (2 * piece)
-    occ = occupancy[0].astype(jnp.float32)
-    slice_total = group * slices
-    prm = jnp.stack(
-        [
-            1.0 - frac_lateral[0],
-            frac_lateral[0],
-            2.0 * lax.reduce_precision(1.0 - frac_vertical[0], 8, 7),
-            2.0 * lax.reduce_precision(frac_vertical[0], 8, 7),
-            extinction[0] * (-0.5 * math.log2(math.e) / slice_total),
-        ]
-    )
     pad_rows = -row_blocks % 8
-    occ_edge = jnp.broadcast_to(jnp.pad(occ[:, -1:], ((0, pad_rows), (0, 0))), (row_blocks + pad_rows, SHIFT))
-    smem = pl.BlockSpec(memory_space=pltpu.SMEM)
+    hbm = pl.BlockSpec(memory_space=pltpu.HBM)
+    small = (
+        occupancy, shear_offsets, frac_lateral, frac_vertical, extinction, view_rank
+    )
     vmem = pl.BlockSpec(memory_space=pltpu.VMEM)
     later = group // 2 - 1
     dma = pltpu.SemaphoreType.DMA
     return pl.pallas_call(
         functools.partial(render_kernel, (slices, rows, cols, group, lanes)),
-        in_specs=[pl.BlockSpec(memory_space=pl.ANY), vmem, smem, smem, smem, smem, smem],
+        in_specs=[hbm] * 7 + [pl.BlockSpec(memory_space=pltpu.SMEM)],
         out_specs=[vmem, vmem],
         out_shape=[jax.ShapeDtypeStruct((piece, cols), jnp.float32)] * 2,
-        scratch_shapes=[
+        scratch_shapes=[pltpu.SMEM(value.shape, value.dtype) for value in small]
+        + [
             pltpu.VMEM((slices, rows, cols), jnp.bfloat16),
             pltpu.VMEM((slices, rows, SHIFT), jnp.bfloat16),
             pltpu.VMEM((row_blocks + pad_rows, SHIFT), jnp.float32),
+            pltpu.VMEM((row_blocks + pad_rows, SHIFT), jnp.float32),
             pltpu.VMEM((slices, 2 * SHIFT, SHIFT), jnp.bfloat16),
+            pltpu.VMEM((2, slices, HALO, SHIFT), jnp.float32),
             pltpu.VMEM((2, group // 2, piece, cols), jnp.float32),
             pltpu.VMEM((row_blocks, 2, pairs, piece, cols), jnp.int16),
             pltpu.VMEM((row_blocks, 2, pairs, piece, cols), jnp.int16),
@@ -330,11 +367,12 @@
             dma((row_blocks,)),
             dma((later,)),
             dma((later,)),
+            dma((len(small),)),
         ],
         compiler_params=pltpu.CompilerParams(
-            collective_id=0, has_side_effects=True, vmem_limit_bytes=48 * 2**20
+            collective_id=0, has_side_effects=True, vmem_limit_bytes=67_043_328
         ),
-    )(voxels, occ_edge, occ, shear_offsets, prm, slab_gain, view_rank)
+    )(voxels, *small, slab_gain)
 
 
 def solution(mesh):

time: 52.3 us -> 48.5 us (0.927)
  other arithmetic: 2.02 us -> 0 us
  Pallas kernels: 45.2 us -> 43.9 us
    pallas_call x1, Pallas kernels: 45.2 us -> 43.9 us  [shards(): pl.pallas_call(functools.partial(render_kernel, (slices, rows, cols, grou...]
    convert_element_type x1 -> x0, other arithmetic: 0.68 us -> none  [shards(): occ = occupancy[0].astype(jnp.float32)]
    mul x1 -> x0, other arithmetic: 0.68 us -> none  [shards(): 2.0 * lax.reduce_precision(frac_vertical[0], 8, 7)]
    another operation x1 -> x0, local copies, waits for them, and re-layouts: 0.67 us -> none  [shards(): jnp.stack([1.0 - frac_lateral[0], frac_lateral[0], 2.0 * lax.reduce_preci...]
    sub x1 -> x0, other arithmetic: 0.66 us -> none  [shards(): 1.0 - frac_lateral[0]]
    unnamed x6 -> x2, local copies, waits for them, and re-layouts: 2.62 us -> 3.14 us
where the time goes in v3:
time: 48.5 us; the launch traced here: 48.3 us
  Pallas kernels  43.9 us (91%)
  local copies, waits for them, and re-layouts  3.14 us (6%)
  between operations  1.29 us (3%)
    pallas_call x1, Pallas kernels, shards(): pl.pallas_call(functools.partial(render_kernel, (slices, rows, cols, grou...  43.9 us
    unnamed x2, local copies, waits for them, and re-layouts  3.14 us

profile of v3, /device:TPU:2, one launch (start us, length us, event | category | flops | bytes accessed | tf_op | source)
XLA Modules:
  0.0 48.3 jit_solution(4585411225598482151)
XLA Ops:
  1.3 43.9 %shard_map.95 = (f32[64,512]{1,0:T(8,128)}, f32[64,512]{1,0:T(8,128)}) custom-call(bf16[16,512,512]{2,1,0:T(8,128)(2,1)} %bitcast.1, s32[1,4,4]{2,1,0:T(4,128)} %occupancy_in.1, s32[1,16]{1,0:T(1,128)} %off_in.1, f32[1,16]{1,0:T(1,128)} %frac_lateral_in.1, f32[1,16]{1,0:T(1,128)} %frac_vertical_in.1, f32[1,16]{1,0:T(1,128)} %extinction_in.1, s32[8]{0:T(128)} %rank_in.1, ...), custom_call_target="tpu_custom_call" | custom-call | tf_op jit(solution)/shard_map/pallas_call | solution.py:343
  45.2 1.6 %copy.13 = f32[64,512]{1,0:T(8,128)} copy(f32[64,512]{1,0:T(8,128)} %get-tuple-element.4) | data formatting | bytes 262144
  46.8 1.6 %copy.14 = f32[64,512]{1,0:T(8,128)} copy(f32[64,512]{1,0:T(8,128)} %get-tuple-element.5) | data formatting | bytes 262144
